TPU v7x, 32 devices: a whole 2x2x4 slice. The times are simulated.
32 devices in a mesh: grp: 2 (over core), dev: 16 (over z, y, x).
Axes of the slice: x: 2, y: 2, z: 4, core: 2. Of those that a mesh axis runs over, the one named last changes fastest.
Arguments:
- coarse_emb: bfloat16 [16384, 128], P('dev'), may hold values from -6 to 6
- req_ids: int32 [16, 2, 16, 16], P('dev', 'grp'), may hold values from 0 to 1023, as said below
- fine_slot: int32 [16, 2, 2048], P('dev', 'grp'), may hold values from 0 to 255, as said below
- tiles: bfloat16 [512, 2, 8, 128, 128], P('dev', 'grp'), may hold values from -0.125 to 0.125
- tile_cols: int32 [512, 2, 8], P('dev', 'grp'), may hold values from 0 to 47
Outputs:
- smoothed: bfloat16 [65536, 128], P('dev')
Inputs may be any that keep to these rules, and one draw needn't show every extreme that they name: For each d, g and o only the first entries of req_ids[d, g, o] are requested, at most 16 of them, and for each d and g some owner o has all 16; the remaining entries are 0. fine_slot[d, g, i] = o * 16 + j always names a requested entry j of req_ids[d, g, o], and every requested entry is named by some fine node.
All inputs are finite; a program needn't handle non-finite values.
Results may differ from a plain program's by a relative error of at most 0.001.
Values may be sent and summed in bfloat16 or wider, within the bound.
A program may use at most 64 MiB of HBM per device.

v0:
```python
import jax
import jax.numpy as jnp
from jax import lax
from jax.sharding import PartitionSpec as P


def with_halo(shard, sides, width):
    for axis, dim in sides:
        count, length = (lax.axis_size(axis), shard.shape[dim])
        up = [(i, (i + 1) % count) for i in range(count - 1)]
        down = [(j, i) for i, j in up]
        last = lax.slice_in_dim(shard, length - width, length, axis=dim)
        initial = lax.slice_in_dim(shard, 0, width, axis=dim)
        before = lax.ppermute(last, axis, up)
        after = lax.ppermute(initial, axis, down)
        shard = jnp.concatenate([before, shard, after], axis=dim)
    return shard


def per_device(coarse_emb, req_ids, fine_slot, tiles, tile_cols):
    owners = lax.axis_size("dev")
    slot_count = req_ids.shape[3]
    feature_dim = coarse_emb.shape[1]
    half_rows = fine_slot.shape[2]
    tile_rows = tiles.shape[3]
    fine_rows = tiles.shape[0] * tile_rows
    wanted_rows = jnp.take(
        coarse_emb, lax.all_to_all(req_ids, "dev", split_axis=2, concat_axis=0, tiled=True), axis=0
    )
    received = lax.all_to_all(wanted_rows, "dev", split_axis=0, concat_axis=2, tiled=True)
    slot_table = received.reshape(owners * slot_count, feature_dim)
    rows_per = min(512, half_rows)
    block_count = half_rows // rows_per
    columns = lax.iota(jnp.int32, owners * slot_count)

    def lift_block(slot_block):
        onehot = (slot_block[:, None] == columns[None, :]).astype(jnp.bfloat16)
        return jnp.dot(onehot, slot_table, preferred_element_type=jnp.float32).astype(jnp.bfloat16)

    lifted = lax.map(lift_block, fine_slot.reshape(block_count, rows_per)).reshape(
        half_rows, feature_dim
    )
    extended = with_halo(lifted, (("dev", 0),), half_rows)
    ext_blocks = extended.reshape(3 * half_rows // tile_rows, tile_rows, feature_dim)
    picked = ext_blocks[tile_cols[:, 0, :]]
    tile_sums = jnp.einsum(
        "rtij,rtjw->riw", tiles[:, 0], picked, preferred_element_type=jnp.float32
    )
    tile_sums = tile_sums.reshape(fine_rows, feature_dim)
    group = lax.axis_index("grp")
    own_part = lax.dynamic_update_slice(
        jnp.zeros((fine_rows, feature_dim), jnp.float32),
        lifted.astype(jnp.float32),
        (group * half_rows, 0),
    )
    partial_value = own_part - 0.5 * tile_sums
    summed = lax.psum(partial_value, "grp")
    return summed.astype(jnp.bfloat16)


def solution(mesh):
    return jax.shard_map(
        per_device,
        mesh=mesh,
        in_specs=(
            P("dev", None),
            P("dev", "grp", None, None),
            P("dev", "grp", None),
            P("dev", "grp", None, None, None),
            P("dev", "grp", None),
        ),
        out_specs=P("dev", None),
        check_vma=False,
    )
```

profile of v0, /device:TPU:0, one launch (start us, length us, event | category | flops | bytes accessed | tf_op | source)
XLA Modules:
  0.0 80.5 jit_solution(1592626263066014495)
XLA Ops:
  0.0 0.0 copy-start
  0.0 8.5 %all-to-all-start = ((s32[1,1,16,16]{3,1,0,2:T(1,128)}), s32[1,1,16,16]{3,1,0,2:T(1,128)S(1)}, u32[]{:S(2)}, u32[]{:S(2)}) async-start(s32[1,1,16,16]{3,1,0,2:T(1,128)} %bitcast.54), calls=%async_computation | async-start | bytes 16384 | tf_op jit(solution)/shard_map/all_to_all | solution.py:28
  8.5 0.5 broadcast.89
  9.0 1.4 %reduce.3 = s32[2048]{0:T(1024)S(1)} reduce(s32[1,1,2048]{2,1,0:T(1,128)} %param.9, s32[]{:T(128)} %broadcast.89), dimensions={0,1}, to_apply=%param.9.reduce_sub_computation.3 | reduce | bytes 16388 | tf_op args[2]
  10.4 5.3 %all-to-all-done = s32[1,1,16,16]{3,1,0,2:T(1,128)S(1)} async-done(((s32[1,1,16,16]{3,1,0,2:T(1,128)}), s32[1,1,16,16]{3,1,0,2:T(1,128)S(1)}, u32[]{:S(2)}, u32[]{:S(2)}) %all-to-all-start) | async-done | bytes 1056 | tf_op jit(solution)/shard_map/all_to_all | solution.py:28
  15.7 0.1 reshape.137
  15.8 0.0 copy-done
  15.8 0.9 %gather_fusion = bf16[256,128]{1,0:T(8,128)(2,1)S(1)} fusion(bf16[1024,128]{1,0:T(8,128)(2,1)S(1)} %copy-done, s32[1024]{0:T(1024)S(1)} %pad_clamp_fusion.1), kind=kCustom, calls=%fused_computation | custom fusion | bytes 132096 | tf_op jit(solution)/shard_map/jit(_take)/gather | solution.py:27
  16.7 0.7 broadcast_select_fusion
  17.4 3.5 %all-to-all-start.1 = ((bf16[16,1,1,16,128]{4,3,2,1,0:T(8,128)(2,1)}), bf16[16,1,1,16,128]{4,3,2,1,0:T(8,128)(2,1)S(1)}, u32[]{:S(2)}, u32[]{:S(2)}) async-start(bf16[16,1,1,16,128]{4,3,2,1,0:T(8,128)(2,1)} %broadcast_select_fusion), calls=%async_computation.1 | async-start | bytes 131072 | tf_op jit(solution)/shard_map/all_to_all | solution.py:30
  20.9 0.7 compare_select_fusion.2
  21.6 0.1 copy.9
  21.7 0.1 reshape.145
  21.8 6.6 %all-to-all-done.1 = bf16[16,1,1,16,128]{4,3,2,1,0:T(8,128)(2,1)S(1)} async-done(((bf16[16,1,1,16,128]{4,3,2,1,0:T(8,128)(2,1)}), bf16[16,1,1,16,128]{4,3,2,1,0:T(8,128)(2,1)S(1)}, u32[]{:S(2)}, u32[]{:S(2)}) %all-to-all-start.1) | async-done | bytes 65568 | tf_op jit(solution)/shard_map/all_to_all | solution.py:30
  28.4 1.3 %while.11 = (s32[]{:T(128)}, bf16[4,512,128]{2,1,0:T(8,128)(2,1)S(1)}, s32[4,512]{1,0:T(4,128)S(1)}, bf16[256,128]{1,0:T(8,128)(2,1)S(1)}, s32[]{:T(128)}) while((s32[]{:T(128)}, bf16[4,512,128]{2,1,0:T(8,128)(2,1)S(1)}, s32[4,512]{1,0:T(4,128)S(1)}, bf16[256,128]{1,0:T(8,128)(2,1)S(1)}, s32[]{:T(128)}) %tuple.24), condition=%wide.region_1.2_spmd.clone, body=%wide.region_0.1_spmd.clone.sunk | while | flops 33751040 | bytes 202821 | solution.py:40
  28.4 0.3 fusion.14
  28.8 0.3 fusion.14
  29.1 0.3 fusion.14
  29.4 0.3 fusion.14
  29.7 2.8 %collective-permute-start = (bf16[2048,128]{1,0:T(8,128)(2,1)S(1)}, bf16[2048,128]{1,0:T(8,128)(2,1)S(1)}, u32[]{:S(2)}, u32[]{:S(2)}) collective-permute-start(bf16[2048,128]{1,0:T(8,128)(2,1)S(1)} %bitcast.45), channel_id=1, source_target_pairs={{0,1},{1,2},{2,3},{3,4},{4,5},{5,6},{6,7},{7,8},{8,9},{9,10},{10,1... | collective-permute-start | bytes 1572872 | tf_op jit(solution)/shard_map/ppermute | solution.py:14
  32.5 1.3 %collective-permute-start.1 = (bf16[2048,128]{1,0:T(8,128)(2,1)S(1)}, bf16[2048,128]{1,0:T(8,128)(2,1)S(1)}, u32[]{:S(2)}, u32[]{:S(2)}) collective-permute-start(bf16[2048,128]{1,0:T(8,128)(2,1)S(1)} %bitcast.46), channel_id=1, source_target_pairs={{1,0},{2,1},{3,2},{4,3},{5,4},{6,5},{7,6},{8,7},{9,8},{10,9},{11,1... | collective-permute-start | bytes 1572872 | tf_op jit(solution)/shard_map/ppermute | solution.py:15
  33.8 0.1 broadcast_in_dim.23
  34.0 0.1 convert_dynamic-update-slice_fusion
  34.0 0.0 copy-start.1
  34.0 18.2 %collective-permute-done = bf16[2048,128]{1,0:T(8,128)(2,1)S(1)} collective-permute-done((bf16[2048,128]{1,0:T(8,128)(2,1)S(1)}, bf16[2048,128]{1,0:T(8,128)(2,1)S(1)}, u32[]{:S(2)}, u32[]{:S(2)}) %collective-permute-start) | collective-permute-done | bytes 524320 | tf_op jit(solution)/shard_map/ppermute | solution.py:14
  52.3 0.0 copy-done.1
  52.3 1.7 %collective-permute-done.1 = bf16[2048,128]{1,0:T(8,128)(2,1)S(1)} collective-permute-done((bf16[2048,128]{1,0:T(8,128)(2,1)S(1)}, bf16[2048,128]{1,0:T(8,128)(2,1)S(1)}, u32[]{:S(2)}, u32[]{:S(2)}) %collective-permute-start.1) | collective-permute-done | bytes 524320 | tf_op jit(solution)/shard_map/ppermute | solution.py:15
  54.0 0.1 pad_maximum_fusion
  54.1 8.6 %gather_fusion.1 = bf16[256,128,128]{2,1,0:T(8,128)(2,1)} fusion(bf16[48,128,128]{2,1,0:T(8,128)(2,1)S(1)} %bitcast.43, s32[1024]{0:T(1024)S(1)} %pad_clamp_fusion), kind=kCustom, calls=%fused_computation.1 | custom fusion | bytes 16778240 | tf_op jit(solution)/shard_map/gather | solution.py:45
  62.7 8.3 %bitcast_multiply_fusion = f32[32,128,128]{1,2,0:T(8,128)S(1)} fusion(bf16[32,8,128,128]{3,2,1,0:T(8,128)(2,1)} %bitcast.44, bf16[32,1,8,128,128]{4,3,2,1,0:T(8,128)(2,1)} %param.10), kind=kOutput, calls=%fused_computation.12 | convolution fusion | flops 1074266112 | bytes 18874368 | tf_op jit(solution)/shard_map/rtij,rtjw->riw/dot_general | solution.py:46
  71.0 0.2 bitcast_subtract_fusion
  71.2 9.3 %all-reduce.1 = bf16[4096,128]{1,0:T(8,128)(2,1)} all-reduce(f32[4096,128]{1,0:T(8,128)S(1)} %bitcast_subtract_fusion), channel_id=1, replica_groups=mesh['grp'=2,'dev'=16] {'grp'}, use_global_device_ids=true, to_apply=%region_2.3 | all-reduce | flops 524288 | bytes 3145728 | tf_op jit(solution)/shard_map/psum | solution.py:57
  (12 shorter events, 0.1 us)
Async XLA Ops:
  0.0 15.8 %copy-start = (bf16[1024,128]{1,0:T(8,128)(2,1)S(1)}, bf16[1024,128]{1,0:T(8,128)(2,1)}, u32[]{:S(2)}) copy-start(bf16[1024,128]{1,0:T(8,128)(2,1)} %param.7) | copy-start | bytes 786436
  0.0 15.7 %all-to-all-start = ((s32[1,1,16,16]{3,1,0,2:T(1,128)}), s32[1,1,16,16]{3,1,0,2:T(1,128)S(1)}, u32[]{:S(2)}, u32[]{:S(2)}) async-start(s32[1,1,16,16]{3,1,0,2:T(1,128)} %bitcast.54), calls=%async_computation | async-start | bytes 16384 | tf_op jit(solution)/shard_map/all_to_all | solution.py:28
  17.4 11.0 %all-to-all-start.1 = ((bf16[16,1,1,16,128]{4,3,2,1,0:T(8,128)(2,1)}), bf16[16,1,1,16,128]{4,3,2,1,0:T(8,128)(2,1)S(1)}, u32[]{:S(2)}, u32[]{:S(2)}) async-start(bf16[16,1,1,16,128]{4,3,2,1,0:T(8,128)(2,1)} %broadcast_select_fusion), calls=%async_computation.1 | async-start | bytes 131072 | tf_op jit(solution)/shard_map/all_to_all | solution.py:30
  29.7 22.6 %collective-permute-start = (bf16[2048,128]{1,0:T(8,128)(2,1)S(1)}, bf16[2048,128]{1,0:T(8,128)(2,1)S(1)}, u32[]{:S(2)}, u32[]{:S(2)}) collective-permute-start(bf16[2048,128]{1,0:T(8,128)(2,1)S(1)} %bitcast.45), channel_id=1, source_target_pairs={{0,1},{1,2},{2,3},{3,4},{4,5},{5,6},{6,7},{7,8},{8,9},{9,10},{10,1... | collective-permute-start | bytes 1572872 | tf_op jit(solution)/shard_map/ppermute | solution.py:14
  32.5 21.5 %collective-permute-start.1 = (bf16[2048,128]{1,0:T(8,128)(2,1)S(1)}, bf16[2048,128]{1,0:T(8,128)(2,1)S(1)}, u32[]{:S(2)}, u32[]{:S(2)}) collective-permute-start(bf16[2048,128]{1,0:T(8,128)(2,1)S(1)} %bitcast.46), channel_id=1, source_target_pairs={{1,0},{2,1},{3,2},{4,3},{5,4},{6,5},{7,6},{8,7},{9,8},{10,9},{11,1... | collective-permute-start | bytes 1572872 | tf_op jit(solution)/shard_map/ppermute | solution.py:15
  34.0 18.2 %copy-start.1 = (f32[4096,128]{1,0:T(8,128)}, f32[4096,128]{1,0:T(8,128)S(1)}, u32[]{:S(2)}) copy-start(f32[4096,128]{1,0:T(8,128)S(1)} %convert_dynamic-update-slice_fusion) | copy-start | bytes 6291460
  62.7 8.3 %copy-start.2 = (f32[4096,128]{1,0:T(8,128)S(1)}, f32[4096,128]{1,0:T(8,128)}, u32[]{:S(2)}) copy-start(f32[4096,128]{1,0:T(8,128)} %copy-done.1) | copy-start | bytes 6291460
where the time goes:
time: 80.9 us; the launch traced here: 80.5 us
  waiting for transfers between devices  31.9 us (39%)
  starting transfers between devices  16 us (20%)
  local copies, waits for them, and re-layouts  10.4 us (13%)
  matrix products  9.4 us (12%)
  blocking collectives  9.29 us (11%)
  other arithmetic  3.2 us (4%)
    ppermute x1, waiting for transfers between devices, with_halo(): before = lax.ppermute(last, axis, up)  18.2 us
    psum x1, blocking collectives, per_device(): summed = lax.psum(partial_value, 'grp')  9.29 us
    gather x1, local copies, waits for them, and re-layouts, per_device(): picked = ext_blocks[tile_cols[:, 0, :]]  8.6 us
    all_to_all x1, starting transfers between devices, per_device(): lax.all_to_all(req_ids, 'dev', split_axis=2, concat_axis=0, tiled=True)  8.47 us
    dot_general x1, matrix products, per_device(): jnp.einsum('rtij,rtjw->riw', tiles[:, 0], picked, preferred_element_type=...  8.25 us
    all_to_all x1, waiting for transfers between devices, per_device(): lax.all_to_all(wanted_rows, 'dev', split_axis=0, concat_axis=2, tiled=True)  6.64 us
    all_to_all x1, waiting for transfers between devices, per_device(): lax.all_to_all(req_ids, 'dev', split_axis=2, concat_axis=0, tiled=True)  5.32 us
    all_to_all x1, starting transfers between devices, per_device(): lax.all_to_all(wanted_rows, 'dev', split_axis=0, concat_axis=2, tiled=True)  3.5 us
  transfers between devices with their start and end apart: 4, of which 4 were waited for; matrix products, arithmetic and copies ran while one was open for 4% of the time, Pallas kernels for 0%

commit v1 on v0

v1 whole, which is shorter than its diff:
```python
import functools

import jax
import jax.numpy as jnp
from jax import lax
from jax.experimental import pallas as pl
from jax.experimental.pallas import tpu as pltpu
from jax.sharding import PartitionSpec as P

MESH = pl.DeviceIdType.MESH
STEP = 4


def kernel(
    n, cap, req_hbm, fs_hbm, coarse_hbm, cols_hbm, tiles_hbm, out_hbm,
    req_v, req_out, req_in, fs, coarse, cols, tiles, rows_pad, tab, onehot, ext,
    part_out, part_in, done,
    local_sem, req_send, req_recv, fs_send, fs_recv, row_send, row_recv,
    part_send, part_recv, fin_send, fin_recv, out_sem,
):
    me = lax.axis_index("dev")
    grp = lax.axis_index("grp")
    other = 1 - grp
    half_blocks = fs.shape[1]
    b = fs.shape[2]
    w = coarse.shape[1]
    slots = n * cap
    steps = half_blocks // STEP

    req_copy = pltpu.make_async_copy(req_hbm, req_v, local_sem.at[0])
    fs_copy = pltpu.make_async_copy(fs_hbm, fs.at[1], local_sem.at[1])
    coarse_copy = pltpu.make_async_copy(coarse_hbm, coarse, local_sem.at[2])
    cols_copy = pltpu.make_async_copy(cols_hbm, cols, local_sem.at[3])
    tiles_copy = pltpu.make_async_copy(tiles_hbm, tiles, local_sem.at[4])
    req_copy.start()
    fs_copy.start()
    coarse_copy.start()
    cols_copy.start()
    tiles_copy.start()

    barrier = pltpu.get_barrier_semaphore()
    pl.semaphore_signal(barrier, inc=1, device_id={"grp": other}, device_id_type=MESH)

    def greet(k, c):
        peer = lax.rem(me + k, n)
        pl.semaphore_signal(barrier, inc=1, device_id={"dev": peer}, device_id_type=MESH)
        return c

    lax.fori_loop(1, n, greet, 0)

    rows_pad[0] = jnp.zeros((cap, w), jnp.bfloat16)
    rows_pad[n + 1] = jnp.zeros((cap, w), jnp.bfloat16)

    @pl.when(me == 0)
    def _():
        fs[0] = jnp.zeros((half_blocks, b), jnp.int32)

    @pl.when(me == n - 1)
    def _():
        fs[2] = jnp.zeros((half_blocks, b), jnp.int32)

    req_copy.wait()

    def spread(o, c):
        req_out[o, :, 0:cap] = req_v[pl.ds(o, 1), :]
        return c

    lax.fori_loop(0, n, spread, 0)
    req_in[me, :, 0:cap] = req_v[pl.ds(me, 1), :]

    def build_onehot(side):
        def one(i, c):
            row = fs[side, pl.ds(i, 1), :].astype(jnp.float32)
            col = jnp.transpose(jnp.broadcast_to(row, (b, b)))
            lanes = lax.broadcasted_iota(jnp.int32, (b, b), 1).astype(jnp.float32)
            base = pl.multiple_of((side * half_blocks + i) * b, b)
            for q in range(slots // b):
                hit = jnp.where(col == lanes + float(q * b), 1.0, 0.0)
                onehot[pl.ds(base, b), q * b:(q + 1) * b] = hit.astype(jnp.bfloat16)
            return c

        lax.fori_loop(0, half_blocks, one, 0)

    fs_copy.wait()
    build_onehot(1)
    pl.semaphore_wait(barrier, n)

    def req_remote(k):
        peer = lax.rem(me + k, n)
        return pltpu.make_async_remote_copy(
            src_ref=req_out.at[peer], dst_ref=req_in.at[me],
            send_sem=req_send.at[k], recv_sem=req_recv.at[me],
            device_id={"dev": peer}, device_id_type=MESH,
        )

    def req_arrival(k):
        peer = lax.rem(me + k, n)
        return pltpu.make_async_remote_copy(
            src_ref=req_out.at[peer], dst_ref=req_in.at[peer],
            send_sem=req_send.at[k], recv_sem=req_recv.at[peer],
            device_id={"dev": peer}, device_id_type=MESH,
        )

    def send_req(k, c):
        req_remote(k).start()
        return c

    lax.fori_loop(1, n, send_req, 0)

    up = pltpu.make_async_remote_copy(
        src_ref=fs.at[1], dst_ref=fs.at[0], send_sem=fs_send.at[0], recv_sem=fs_recv.at[0],
        device_id={"dev": lax.rem(me + 1, n)}, device_id_type=MESH,
    )
    down = pltpu.make_async_remote_copy(
        src_ref=fs.at[1], dst_ref=fs.at[2], send_sem=fs_send.at[1], recv_sem=fs_recv.at[1],
        device_id={"dev": lax.rem(me + n - 1, n)}, device_id_type=MESH,
    )

    @pl.when(me < n - 1)
    def _():
        up.start()

    @pl.when(me > 0)
    def _():
        down.start()

    coarse_copy.wait()

    def wait_req(k, c):
        req_arrival(k).wait_recv()
        return c

    lax.fori_loop(1, n, wait_req, 0)

    owned = coarse.shape[0]
    group = min(16, n)

    def gather(i, c):
        ids = req_in[pl.ds(i * group, group)].astype(jnp.float32)
        ids = jnp.broadcast_to(ids, (group, cap, ids.shape[2]))
        slot = lax.broadcasted_iota(jnp.int32, ids.shape, 1)
        lane = lax.broadcasted_iota(jnp.int32, ids.shape, 2)
        col = jnp.sum(jnp.where(slot == lane, ids, 0.0), axis=2, keepdims=True)
        col = col.reshape(group * cap, 1)
        node = lax.broadcasted_iota(jnp.int32, (group * cap, owned), 1).astype(jnp.float32)
        hit = jnp.where(col == node, 1.0, 0.0).astype(jnp.bfloat16)
        rows = jnp.dot(hit, coarse[...], preferred_element_type=jnp.float32)
        rows_pad[pl.ds(1 + i * group, group)] = rows.astype(jnp.bfloat16).reshape(group, cap, w)
        return c

    lax.fori_loop(0, n // group, gather, 0)

    def row_remote(k):
        peer = lax.rem(me + k, n)
        return pltpu.make_async_remote_copy(
            src_ref=rows_pad.at[pl.ds(peer, 3)], dst_ref=tab.at[me],
            send_sem=row_send.at[k], recv_sem=row_recv.at[me],
            device_id={"dev": peer}, device_id_type=MESH,
        )

    def row_arrival(k):
        peer = lax.rem(me + k, n)
        return pltpu.make_async_remote_copy(
            src_ref=rows_pad.at[pl.ds(peer, 3)], dst_ref=tab.at[peer],
            send_sem=row_send.at[k], recv_sem=row_recv.at[peer],
            device_id={"dev": peer}, device_id_type=MESH,
        )

    def send_rows(k, c):
        row_remote(k).start()
        return c

    lax.fori_loop(1, n, send_rows, 0)
    tab[me] = rows_pad[pl.ds(me, 3)]

    @pl.when(me > 0)
    def _():
        up.wait_recv()

    build_onehot(0)

    @pl.when(me < n - 1)
    def _():
        down.wait_recv()

    build_onehot(2)

    def wait_rows(k, c):
        row_arrival(k).wait_recv()
        return c

    lax.fori_loop(1, n, wait_rows, 0)

    for side in range(3):
        table = tab[:, side].reshape(slots, w)

        def lift(i, c, side=side, table=table):
            first = side * half_blocks + i * STEP
            hits = onehot[pl.ds(pl.multiple_of(first * b, b), STEP * b), :]
            rows = jnp.dot(hits, table, preferred_element_type=jnp.float32)
            ext[pl.ds(first, STEP)] = rows.astype(jnp.bfloat16).reshape(STEP, b, w)
            return c

        lax.fori_loop(0, steps, lift, 0)

    cols_copy.wait()
    tiles_copy.wait()
    tpr = tiles.shape[1]

    def tile_sum(r):
        lhs = jnp.concatenate([tiles[r, t] for t in range(tpr)], axis=1)
        rhs = jnp.concatenate([ext[cols[t, r]] for t in range(tpr)], axis=0)
        return jnp.dot(lhs, rhs, preferred_element_type=jnp.float32)

    def part_copy(i):
        return pltpu.make_async_remote_copy(
            src_ref=part_out.at[pl.ds(i * STEP, STEP)], dst_ref=part_in.at[pl.ds(i * STEP, STEP)],
            send_sem=part_send.at[i], recv_sem=part_recv.at[i],
            device_id={"grp": other}, device_id_type=MESH,
        )

    def give(i, c):
        for j in range(STEP):
            r = i * STEP + j
            part_out[r] = tile_sum(other * half_blocks + r)
        part_copy(i).start()
        return c

    lax.fori_loop(0, steps, give, 0)

    def fin_copy(i):
        rows = pl.ds(grp * half_blocks + i * STEP, STEP)
        return pltpu.make_async_remote_copy(
            src_ref=done.at[rows], dst_ref=done.at[rows],
            send_sem=fin_send.at[i], recv_sem=fin_recv.at[i],
            device_id={"grp": other}, device_id_type=MESH,
        )

    def fin_arrival(i):
        rows = pl.ds(other * half_blocks + i * STEP, STEP)
        return pltpu.make_async_remote_copy(
            src_ref=done.at[rows], dst_ref=done.at[rows],
            send_sem=fin_send.at[i], recv_sem=fin_recv.at[i],
            device_id={"grp": other}, device_id_type=MESH,
        )

    def own_out(i):
        rows = pl.ds(grp * half_blocks + i * STEP, STEP)
        return pltpu.make_async_copy(done.at[rows], out_hbm.at[rows], out_sem.at[0, i])

    def other_out(i):
        rows = pl.ds(other * half_blocks + i * STEP, STEP)
        return pltpu.make_async_copy(done.at[rows], out_hbm.at[rows], out_sem.at[1, i])

    def finish(i, c):
        part_copy(i).wait_recv()
        for j in range(STEP):
            r = i * STEP + j
            total = tile_sum(grp * half_blocks + r) + part_in[r]
            value = ext[half_blocks + r].astype(jnp.float32) - 0.5 * total
            done[grp * half_blocks + r] = value.astype(jnp.bfloat16)
        fin_copy(i).start()
        own_out(i).start()
        return c

    lax.fori_loop(0, steps, finish, 0)

    def collect(i, c):
        fin_arrival(i).wait_recv()
        other_out(i).start()
        return c

    lax.fori_loop(0, steps, collect, 0)

    def drain_peer(k, c):
        req_remote(k).wait_send()
        row_remote(k).wait_send()
        return c

    lax.fori_loop(1, n, drain_peer, 0)

    @pl.when(me < n - 1)
    def _():
        up.wait_send()

    @pl.when(me > 0)
    def _():
        down.wait_send()

    def drain_step(i, c):
        part_copy(i).wait_send()
        fin_copy(i).wait_send()
        own_out(i).wait()
        other_out(i).wait()
        return c

    lax.fori_loop(0, steps, drain_step, 0)


def per_device(coarse_emb, req_ids, fine_slot, tiles, tile_cols):
    n = lax.axis_size("dev")
    cap = req_ids.shape[3]
    owned, w = coarse_emb.shape
    row_blocks, _, tpr, b, _ = tiles.shape
    half_rows = fine_slot.shape[2]
    half_blocks = half_rows // b
    steps = half_blocks // STEP
    slots = n * cap
    dma = pltpu.SemaphoreType.DMA
    out = pl.pallas_call(
        functools.partial(kernel, n, cap),
        out_shape=jax.ShapeDtypeStruct((row_blocks, b, w), jnp.bfloat16),
        in_specs=[pl.BlockSpec(memory_space=pl.ANY)] * 5,
        out_specs=pl.BlockSpec(memory_space=pl.ANY),
        scratch_shapes=[
            pltpu.VMEM((n, cap), jnp.int32),
            pltpu.VMEM((n, 1, 128), jnp.int32),
            pltpu.VMEM((n, 1, 128), jnp.int32),
            pltpu.VMEM((3, half_blocks, b), jnp.int32),
            pltpu.VMEM((owned, w), jnp.bfloat16),
            pltpu.SMEM((tpr, row_blocks), jnp.int32),
            pltpu.VMEM((row_blocks, tpr, b, b), jnp.bfloat16),
            pltpu.VMEM((n + 2, cap, w), jnp.bfloat16),
            pltpu.VMEM((n, 3, cap, w), jnp.bfloat16),
            pltpu.VMEM((3 * half_rows, slots), jnp.bfloat16),
            pltpu.VMEM((3 * half_blocks, b, w), jnp.bfloat16),
            pltpu.VMEM((half_blocks, b, w), jnp.float32),
            pltpu.VMEM((half_blocks, b, w), jnp.float32),
            pltpu.VMEM((row_blocks, b, w), jnp.bfloat16),
            dma((5,)),
            dma((n,)),
            dma((n,)),
            dma((2,)),
            dma((2,)),
            dma((n,)),
            dma((n,)),
            dma((steps,)),
            dma((steps,)),
            dma((steps,)),
            dma((steps,)),
            dma((2, steps)),
        ],
        compiler_params=pltpu.CompilerParams(
            collective_id=0, has_side_effects=True, vmem_limit_bytes=60 * 1024 * 1024
        ),
    )(
        req_ids[0, 0],
        fine_slot.reshape(half_blocks, b),
        coarse_emb,
        tile_cols[:, 0].T,
        tiles[:, 0],
    )
    return out.reshape(row_blocks * b, w)


def solution(mesh):
    return jax.shard_map(
        per_device,
        mesh=mesh,
        in_specs=(
            P("dev", None),
            P("dev", "grp", None, None),
            P("dev", "grp", None),
            P("dev", "grp", None, None, None),
            P("dev", "grp", None),
        ),
        out_specs=P("dev", None),
        check_vma=False,
    )
```

time: 80.9 us -> 27.7 us (0.34)
  waiting for transfers between devices: 31.9 us -> 0 us
  Pallas kernels: 0 us -> 25.2 us
  starting transfers between devices: 16 us -> 0 us
  matrix products: 9.4 us -> 0 us
  blocking collectives: 9.29 us -> 0 us
  local copies, waits for them, and re-layouts: 10.4 us -> 2.26 us
  other arithmetic: 3.2 us -> 0 us
    pallas_call x0 -> x1, Pallas kernels: none -> 25.2 us  [per_device(): pl.pallas_call(functools.partial(kernel, n, cap), out_shape=jax.ShapeDtyp...]
    ppermute x2 -> x0, waiting for transfers between devices: 20 us -> none  [the longest x1 18.2 us: with_halo(): before = lax.ppermute(last, axis, up)]
    all_to_all x2 -> x0, starting transfers between devices: 12 us -> none  [the longest x1 8.47 us: per_device(): lax.all_to_all(req_ids, 'dev', split_axis=2, concat_axis=0, tiled=True)]
    all_to_all x2 -> x0, waiting for transfers between devices: 12 us -> none  [the longest x1 6.64 us: per_device(): lax.all_to_all(wanted_rows, 'dev', split_axis=0, concat_axis=2, tiled=True)]
    gather x2 -> x0, local copies, waits for them, and re-layouts: 9.45 us -> none  [the longest x1 8.6 us: per_device(): picked = ext_blocks[tile_cols[:, 0, :]]]
    dot_general x5 -> x0, matrix products: 9.4 us -> none  [the longest x1 8.25 us: per_device(): jnp.einsum('rtij,rtjw->riw', tiles[:, 0], picked, preferred_element_type=...]
    psum x1 -> x0, blocking collectives: 9.29 us -> none  [per_device(): summed = lax.psum(partial_value, 'grp')]
    ppermute x2 -> x0, starting transfers between devices: 4.06 us -> none  [the longest x1 2.77 us: with_halo(): before = lax.ppermute(last, axis, up)]
  transfers between devices with their start and end apart: 4 -> 0, of which waited for: 4 -> 0; matrix products, arithmetic and copies ran while one was open for 4% -> 0% of each run, Pallas kernels for 0% -> 0%
where the time goes in v1:
time: 27.7 us; the launch traced here: 27.5 us
  Pallas kernels  25.2 us (91%)
  local copies, waits for them, and re-layouts  2.26 us (8%)
    pallas_call x1, Pallas kernels, per_device(): pl.pallas_call(functools.partial(kernel, n, cap), out_shape=jax.ShapeDtyp...  25.2 us
    unnamed x1, local copies, waits for them, and re-layouts  2.26 us

profile of v1, /device:TPU:0, one launch (start us, length us, event | category | flops | bytes accessed | tf_op | source)
XLA Modules:
  0.0 27.5 jit_solution(2394664855293597646)
XLA Ops:
  0.0 25.2 %shard_map.55 = bf16[32,128,128]{2,1,0:T(8,128)(2,1)} custom-call(s32[16,16]{1,0:T(8,128)} %bitcast.9, s32[16,128]{1,0:T(8,128)} %bitcast.10, bf16[1024,128]{1,0:T(8,128)(2,1)} %coarse_hbm.1, s32[8,32]{1,0:T(8,128)} %bitcast.11, bf16[32,8,128,128]{3,2,1,0:T(8,128)(2,1)} %bitcast.7), custom_call_target="tpu_custom_call" | custom-call | tf_op jit(solution)/shard_map/pallas_call | solution.py:310
  25.3 2.3 %copy.7 = bf16[4096,128]{1,0:T(8,128)(2,1)} copy(bf16[4096,128]{1,0:T(8,128)(2,1)} %bitcast.8) | data formatting | bytes 2097152

commit v2 on v1

--- a/solution.py
+++ b/solution.py
@@ -8,15 +8,17 @@
 from jax.sharding import PartitionSpec as P
 
 MESH = pl.DeviceIdType.MESH
-STEP = 4
+LIFT = 16
+GIVE = 4
+KEEP = 4
 
 
 def kernel(
-    n, cap, req_hbm, fs_hbm, coarse_hbm, cols_hbm, tiles_hbm, out_hbm,
+    n, cap, req_hbm, fs_hbm, coarse_hbm, cols_hbm, tiles_hbm, done,
     req_v, req_out, req_in, fs, coarse, cols, tiles, rows_pad, tab, onehot, ext,
-    part_out, part_in, done,
+    part_out, part_in,
     local_sem, req_send, req_recv, fs_send, fs_recv, row_send, row_recv,
-    part_send, part_recv, fin_send, fin_recv, out_sem,
+    part_send, part_recv, fin_send, fin_recv,
 ):
     me = lax.axis_index("dev")
     grp = lax.axis_index("grp")
@@ -25,8 +27,6 @@
     b = fs.shape[2]
     w = coarse.shape[1]
     slots = n * cap
-    steps = half_blocks // STEP
-
     req_copy = pltpu.make_async_copy(req_hbm, req_v, local_sem.at[0])
     fs_copy = pltpu.make_async_copy(fs_hbm, fs.at[1], local_sem.at[1])
     coarse_copy = pltpu.make_async_copy(coarse_hbm, coarse, local_sem.at[2])
@@ -195,13 +195,13 @@
         table = tab[:, side].reshape(slots, w)
 
         def lift(i, c, side=side, table=table):
-            first = side * half_blocks + i * STEP
-            hits = onehot[pl.ds(pl.multiple_of(first * b, b), STEP * b), :]
+            first = side * half_blocks + i * LIFT
+            hits = onehot[pl.ds(pl.multiple_of(first * b, b), LIFT * b), :]
             rows = jnp.dot(hits, table, preferred_element_type=jnp.float32)
-            ext[pl.ds(first, STEP)] = rows.astype(jnp.bfloat16).reshape(STEP, b, w)
+            ext[pl.ds(first, LIFT)] = rows.astype(jnp.bfloat16).reshape(LIFT, b, w)
             return c
 
-        lax.fori_loop(0, steps, lift, 0)
+        lax.fori_loop(0, half_blocks // LIFT, lift, 0)
 
     cols_copy.wait()
     tiles_copy.wait()
@@ -214,22 +214,22 @@
 
     def part_copy(i):
         return pltpu.make_async_remote_copy(
-            src_ref=part_out.at[pl.ds(i * STEP, STEP)], dst_ref=part_in.at[pl.ds(i * STEP, STEP)],
+            src_ref=part_out.at[pl.ds(i * GIVE, GIVE)], dst_ref=part_in.at[pl.ds(i * GIVE, GIVE)],
             send_sem=part_send.at[i], recv_sem=part_recv.at[i],
             device_id={"grp": other}, device_id_type=MESH,
         )
 
     def give(i, c):
-        for j in range(STEP):
-            r = i * STEP + j
+        for j in range(GIVE):
+            r = i * GIVE + j
             part_out[r] = tile_sum(other * half_blocks + r)
         part_copy(i).start()
         return c
 
-    lax.fori_loop(0, steps, give, 0)
+    lax.fori_loop(0, half_blocks // GIVE, give, 0)
 
     def fin_copy(i):
-        rows = pl.ds(grp * half_blocks + i * STEP, STEP)
+        rows = pl.ds(grp * half_blocks + i * KEEP, KEEP)
         return pltpu.make_async_remote_copy(
             src_ref=done.at[rows], dst_ref=done.at[rows],
             send_sem=fin_send.at[i], recv_sem=fin_recv.at[i],
@@ -237,40 +237,29 @@
         )
 
     def fin_arrival(i):
-        rows = pl.ds(other * half_blocks + i * STEP, STEP)
+        rows = pl.ds(other * half_blocks + i * KEEP, KEEP)
         return pltpu.make_async_remote_copy(
             src_ref=done.at[rows], dst_ref=done.at[rows],
             send_sem=fin_send.at[i], recv_sem=fin_recv.at[i],
             device_id={"grp": other}, device_id_type=MESH,
         )
 
-    def own_out(i):
-        rows = pl.ds(grp * half_blocks + i * STEP, STEP)
-        return pltpu.make_async_copy(done.at[rows], out_hbm.at[rows], out_sem.at[0, i])
-
-    def other_out(i):
-        rows = pl.ds(other * half_blocks + i * STEP, STEP)
-        return pltpu.make_async_copy(done.at[rows], out_hbm.at[rows], out_sem.at[1, i])
-
     def finish(i, c):
-        part_copy(i).wait_recv()
-        for j in range(STEP):
-            r = i * STEP + j
+        if KEEP < GIVE:
+            @pl.when(lax.rem(i, GIVE // KEEP) == 0)
+            def _():
+                part_copy(i // (GIVE // KEEP)).wait_recv()
+        else:
+            part_copy(i).wait_recv()
+        for j in range(KEEP):
+            r = i * KEEP + j
             total = tile_sum(grp * half_blocks + r) + part_in[r]
             value = ext[half_blocks + r].astype(jnp.float32) - 0.5 * total
             done[grp * half_blocks + r] = value.astype(jnp.bfloat16)
         fin_copy(i).start()
-        own_out(i).start()
-        return c
-
-    lax.fori_loop(0, steps, finish, 0)
-
-    def collect(i, c):
-        fin_arrival(i).wait_recv()
-        other_out(i).start()
-        return c
-
-    lax.fori_loop(0, steps, collect, 0)
+        return c
+
+    lax.fori_loop(0, half_blocks // KEEP, finish, 0)
 
     def drain_peer(k, c):
         req_remote(k).wait_send()
@@ -287,14 +276,18 @@
     def _():
         down.wait_send()
 
-    def drain_step(i, c):
+    def drain_give(i, c):
         part_copy(i).wait_send()
+        return c
+
+    lax.fori_loop(0, half_blocks // GIVE, drain_give, 0)
+
+    def drain_keep(i, c):
         fin_copy(i).wait_send()
-        own_out(i).wait()
-        other_out(i).wait()
-        return c
-
-    lax.fori_loop(0, steps, drain_step, 0)
+        fin_arrival(i).wait_recv()
+        return c
+
+    lax.fori_loop(0, half_blocks // KEEP, drain_keep, 0)
 
 
 def per_device(coarse_emb, req_ids, fine_slot, tiles, tile_cols):
@@ -304,14 +297,14 @@
     row_blocks, _, tpr, b, _ = tiles.shape
     half_rows = fine_slot.shape[2]
     half_blocks = half_rows // b
-    steps = half_blocks // STEP
+    gives, keeps = half_blocks // GIVE, half_blocks // KEEP
     slots = n * cap
     dma = pltpu.SemaphoreType.DMA
     out = pl.pallas_call(
         functools.partial(kernel, n, cap),
-        out_shape=jax.ShapeDtypeStruct((row_blocks, b, w), jnp.bfloat16),
+        out_shape=pltpu.VMEM((row_blocks, b, w), jnp.bfloat16),
         in_specs=[pl.BlockSpec(memory_space=pl.ANY)] * 5,
-        out_specs=pl.BlockSpec(memory_space=pl.ANY),
+        out_specs=pl.BlockSpec(memory_space=pltpu.VMEM),
         scratch_shapes=[
             pltpu.VMEM((n, cap), jnp.int32),
             pltpu.VMEM((n, 1, 128), jnp.int32),
@@ -326,7 +319,6 @@
             pltpu.VMEM((3 * half_blocks, b, w), jnp.bfloat16),
             pltpu.VMEM((half_blocks, b, w), jnp.float32),
             pltpu.VMEM((half_blocks, b, w), jnp.float32),
-            pltpu.VMEM((row_blocks, b, w), jnp.bfloat16),
             dma((5,)),
             dma((n,)),
             dma((n,)),
@@ -334,22 +326,24 @@
             dma((2,)),
             dma((n,)),
             dma((n,)),
-            dma((steps,)),
-            dma((steps,)),
-            dma((steps,)),
-            dma((steps,)),
-            dma((2, steps)),
+            dma((gives,)),
+            dma((gives,)),
+            dma((keeps,)),
+            dma((keeps,)),
         ],
         compiler_params=pltpu.CompilerParams(
-            collective_id=0, has_side_effects=True, vmem_limit_bytes=60 * 1024 * 1024
+            collective_id=0, has_side_effects=True, vmem_limit_bytes=48 * 1024 * 1024
         ),
-    )(
-        req_ids[0, 0],
-        fine_slot.reshape(half_blocks, b),
-        coarse_emb,
-        tile_cols[:, 0].T,
-        tiles[:, 0],
-    )
+    )(*(
+        pltpu.with_memory_space_constraint(x, pltpu.HBM)
+        for x in (
+            req_ids[0, 0],
+            fine_slot.reshape(half_blocks, b),
+            coarse_emb,
+            tile_cols[:, 0].T,
+            tiles[:, 0],
+        )
+    ))
     return out.reshape(row_blocks * b, w)
 
 

time: 27.7 us -> 24 us (0.87)
  Pallas kernels: 25.2 us -> 22.8 us
  local copies, waits for them, and re-layouts: 2.26 us -> 0.97 us
    pallas_call x1, Pallas kernels: 25.2 us -> 22.8 us  [per_device(): pl.pallas_call(functools.partial(kernel, n, cap), out_shape=pltpu.VMEM((r...]
    unnamed x1, local copies, waits for them, and re-layouts: 2.26 us -> 0.97 us
where the time goes in v2:
time: 24 us; the launch traced here: 23.7 us
  Pallas kernels  22.8 us (95%)
  local copies, waits for them, and re-layouts  0.97 us (4%)
    pallas_call x1, Pallas kernels, per_device(): pl.pallas_call(functools.partial(kernel, n, cap), out_shape=pltpu.VMEM((r...  22.8 us
    unnamed x1, local copies, waits for them, and re-layouts  0.97 us

profile of v2, /device:TPU:0, one launch (start us, length us, event | category | flops | bytes accessed | tf_op | source)
XLA Modules:
  0.0 23.7 jit_solution(1643492173156976617)
XLA Ops:
  0.0 22.8 %shard_map.55 = bf16[32,128,128]{2,1,0:T(8,128)(2,1)S(1)} custom-call(s32[16,16]{1,0:T(8,128)} %bitcast.9, s32[16,128]{1,0:T(8,128)} %bitcast.10, bf16[1024,128]{1,0:T(8,128)(2,1)} %coarse_hbm.1, s32[8,32]{1,0:T(8,128)} %bitcast.11, bf16[32,8,128,128]{3,2,1,0:T(8,128)(2,1)} %bitcast.8), custom_call_target="tpu_custom_call" | custom-call | tf_op jit(solution)/shard_map/pallas_call | solution.py:303
  22.8 1.0 %copy.7 = bf16[4096,128]{1,0:T(8,128)(2,1)} copy(bf16[4096,128]{1,0:T(8,128)(2,1)S(1)} %bitcast.7) | data formatting | bytes 2097152

commit v3 on v2

--- a/solution.py
+++ b/solution.py
@@ -11,6 +11,18 @@
 LIFT = 16
 GIVE = 4
 KEEP = 4
+
+
+def wrapped(index, n):
+    return jnp.where(index >= n, index - n, index)
+
+
+def each_peer(n, body):
+    if n <= 16:
+        for k in range(1, n):
+            body(k, 0)
+    else:
+        lax.fori_loop(1, n, body, 0)
 
 
 def kernel(
@@ -42,11 +54,11 @@
     pl.semaphore_signal(barrier, inc=1, device_id={"grp": other}, device_id_type=MESH)
 
     def greet(k, c):
-        peer = lax.rem(me + k, n)
+        peer = wrapped(me + k, n)
         pl.semaphore_signal(barrier, inc=1, device_id={"dev": peer}, device_id_type=MESH)
         return c
 
-    lax.fori_loop(1, n, greet, 0)
+    each_peer(n, greet)
 
     rows_pad[0] = jnp.zeros((cap, w), jnp.bfloat16)
     rows_pad[n + 1] = jnp.zeros((cap, w), jnp.bfloat16)
@@ -86,7 +98,7 @@
     pl.semaphore_wait(barrier, n)
 
     def req_remote(k):
-        peer = lax.rem(me + k, n)
+        peer = wrapped(me + k, n)
         return pltpu.make_async_remote_copy(
             src_ref=req_out.at[peer], dst_ref=req_in.at[me],
             send_sem=req_send.at[k], recv_sem=req_recv.at[me],
@@ -94,7 +106,7 @@
         )
 
     def req_arrival(k):
-        peer = lax.rem(me + k, n)
+        peer = wrapped(me + k, n)
         return pltpu.make_async_remote_copy(
             src_ref=req_out.at[peer], dst_ref=req_in.at[peer],
             send_sem=req_send.at[k], recv_sem=req_recv.at[peer],
@@ -105,7 +117,7 @@
         req_remote(k).start()
         return c
 
-    lax.fori_loop(1, n, send_req, 0)
+    each_peer(n, send_req)
 
     up = pltpu.make_async_remote_copy(
         src_ref=fs.at[1], dst_ref=fs.at[0], send_sem=fs_send.at[0], recv_sem=fs_recv.at[0],
@@ -151,7 +163,7 @@
     lax.fori_loop(0, n // group, gather, 0)
 
     def row_remote(k):
-        peer = lax.rem(me + k, n)
+        peer = wrapped(me + k, n)
         return pltpu.make_async_remote_copy(
             src_ref=rows_pad.at[pl.ds(peer, 3)], dst_ref=tab.at[me],
             send_sem=row_send.at[k], recv_sem=row_recv.at[me],
@@ -159,7 +171,7 @@
         )
 
     def row_arrival(k):
-        peer = lax.rem(me + k, n)
+        peer = wrapped(me + k, n)
         return pltpu.make_async_remote_copy(
             src_ref=rows_pad.at[pl.ds(peer, 3)], dst_ref=tab.at[peer],
             send_sem=row_send.at[k], recv_sem=row_recv.at[peer],
@@ -170,7 +182,7 @@
         row_remote(k).start()
         return c
 
-    lax.fori_loop(1, n, send_rows, 0)
+    each_peer(n, send_rows)
     tab[me] = rows_pad[pl.ds(me, 3)]
 
     @pl.when(me > 0)

time: 24 us -> 24 us (level)
  no operation moved by 1% of the time
where the time goes in v3:
time: 24 us; the launch traced here: 23.7 us
  Pallas kernels  22.8 us (95%)
  local copies, waits for them, and re-layouts  0.97 us (4%)
    pallas_call x1, Pallas kernels, per_device(): pl.pallas_call(functools.partial(kernel, n, cap), out_shape=pltpu.VMEM((r...  22.8 us
    unnamed x1, local copies, waits for them, and re-layouts  0.97 us

profile of v3, /device:TPU:0, one launch (start us, length us, event | category | flops | bytes accessed | tf_op | source)
XLA Modules:
  0.0 23.7 jit_solution(12053775282518880656)
XLA Ops:
  0.0 22.8 %shard_map.55 = bf16[32,128,128]{2,1,0:T(8,128)(2,1)S(1)} custom-call(s32[16,16]{1,0:T(8,128)} %bitcast.9, s32[16,128]{1,0:T(8,128)} %bitcast.10, bf16[1024,128]{1,0:T(8,128)(2,1)} %coarse_hbm.1, s32[8,32]{1,0:T(8,128)} %bitcast.11, bf16[32,8,128,128]{3,2,1,0:T(8,128)(2,1)} %bitcast.8), custom_call_target="tpu_custom_call" | custom-call | tf_op jit(solution)/shard_map/pallas_call | solution.py:315
  22.8 1.0 %copy.7 = bf16[4096,128]{1,0:T(8,128)(2,1)} copy(bf16[4096,128]{1,0:T(8,128)(2,1)S(1)} %bitcast.7) | data formatting | bytes 2097152
